TPU v7x, 512 devices: a whole 4x8x8 slice. The times are simulated.
512 devices in a mesh: gx: 16 (over y_hi, z), gy: 4 (over y_lo), gz: 8 (over x, core).
Axes of the slice: x: 4, y: 8 (y_hi: 2, y_lo: 4; y = y_hi * 4 + y_lo), z: 8, core: 2. Of those that a mesh axis runs over, the one named last changes fastest.
Arguments:
- pair: bfloat16 [512, 512, 128], P('gx', ('gy', 'gz')), may hold values from -6 to 6
- pair_mask: int32 [512, 512], P('gx', ('gy', 'gz')), may hold values 0 or 1
- in_gain: float32 [128], replicated, may hold values from 0.1 to 1.9
- in_bias: float32 [128], replicated, may hold values from -3 to 3
- proj_weight: bfloat16 [128, 512], replicated, may hold values from -0.5 to 0.5
- gate_weight: bfloat16 [128, 128], replicated, may hold values from -0.5 to 0.5
- out_gain: float32 [128], replicated, may hold values from 0.1 to 1.9
- out_bias: float32 [128], replicated, may hold values from -3 to 3
- out_weight: bfloat16 [128, 128], replicated, may hold values from -0.5 to 0.5
Outputs:
- update: bfloat16 [512, 512, 128], P('gx', ('gy', 'gz'))
All inputs are finite; a program needn't handle non-finite values. No bound on the sum of `pair_mask` on one device may be relied on, other than what follows from the above.
Results may differ from a plain program's by a relative error of at most 0.0071.
Values may be sent and summed in bfloat16 or wider, within the bound.
A program may use at most 64 MiB of HBM per device.

v0:
```python
import jax
import jax.numpy as jnp
from jax import lax
from jax.sharding import Mesh
from jax.sharding import PartitionSpec as P

GX = ("gx_0", "gx_1")


def sent_to_all(x, axis):
    copies = jnp.broadcast_to(x, (lax.axis_size(axis), *x.shape))
    return lax.all_to_all(copies, axis, split_axis=0, concat_axis=0, tiled=True)


def in_order(tiles, dim):
    tiles = jnp.moveaxis(tiles, 0, dim)
    dims = tiles.shape
    return tiles.reshape(*dims[:dim], dims[dim] * dims[dim + 1], *dims[dim + 2 :])


def gathered_copies(x, axis, dim):
    tiles = sent_to_all(x, axis)
    return in_order(tiles, dim)


def in_one_piece(arrays, axis, dim, along):
    both = jnp.concatenate(arrays, axis=along)
    result, at, gathered = (gathered_copies(both, axis, dim), 0, [])
    for a in arrays:
        gathered.append(lax.slice_in_dim(result, at, at + a.shape[along], axis=along))
        at += a.shape[along]
    return tuple(gathered)


def stacked_from(x, axes, sequence):
    tiles = x
    for k in sequence:
        tiles = lax.all_gather(tiles, axes[k])
    done = sequence[::-1]
    back = [done.index(k) for k in range(len(axes))]
    tiles = tiles.transpose(*back, *range(len(axes), tiles.ndim))
    return tiles.reshape(-1, *x.shape)


def gathered_by_axis(x, axes, sequence, dim):
    return in_order(stacked_from(x, axes, sequence), dim)


def in_blocks(x, dim, size):
    before, after = (x.shape[:dim], x.shape[dim + 1 :])
    return jnp.moveaxis(x.reshape(*before, size, -1, *after), dim, 0)


def sent_and_summed(x, axis, dim):
    size = lax.axis_size(axis)
    tiles = lax.all_to_all(in_blocks(x, dim, size), axis, 0, 0, tiled=True)
    return jnp.sum(tiles.astype(jnp.float32), axis=0)


def normalize(values, gain, bias):
    average = jnp.mean(values, axis=-1, keepdims=True)
    centered = values - average
    variance = jnp.mean(centered * centered, axis=-1, keepdims=True)
    return centered * lax.rsqrt(variance + 1e-05) * gain + bias


def project(tile, mask_value, in_gain, in_bias, proj_weight):
    hidden = proj_weight.shape[1] // 4
    normed = normalize(tile.astype(jnp.float32), in_gain, in_bias).astype(jnp.bfloat16)
    projected = jnp.einsum("rwc,cd->rwd", normed, proj_weight, preferred_element_type=jnp.float32)
    left_side = (
        jax.nn.sigmoid(projected[:, :, :hidden]) * projected[:, :, hidden : 2 * hidden] * mask_value
    ).astype(jnp.bfloat16)
    right_side = (
        jax.nn.sigmoid(projected[:, :, 2 * hidden : 3 * hidden])
        * projected[:, :, 3 * hidden :]
        * mask_value
    ).astype(jnp.bfloat16)
    return (normed, left_side, right_side)


def on_device(
    pair, pair_mask, in_gain, in_bias, proj_weight, gate_weight, out_gain, out_bias, out_weight
):
    mask_value = pair_mask.astype(jnp.float32)[:, :, None]
    normed, left_side, own_right = project(pair, mask_value, in_gain, in_bias, proj_weight)
    left_slab, right_slab = in_one_piece((left_side, own_right), "gy", 1, 0)
    every_row = gathered_by_axis(own_right, GX, (0, 1), 0)
    row_panel = lax.all_to_all(every_row, "gy", split_axis=0, concat_axis=1, tiled=True)
    summed = sent_and_summed(
        jnp.einsum("jkc,ikc->jic", row_panel, left_slab, preferred_element_type=jnp.float32).astype(
            jnp.bfloat16
        ),
        "gz",
        0,
    )
    triangle = jnp.transpose(summed, (1, 0, 2))
    tri_normed = normalize(triangle, out_gain, out_bias).astype(jnp.bfloat16)
    gating = jax.nn.sigmoid(
        jnp.einsum("rwc,cd->rwd", normed, gate_weight, preferred_element_type=jnp.float32)
    )
    mixed = jnp.einsum("rwh,hc->rwc", tri_normed, out_weight, preferred_element_type=jnp.float32)
    return (gating * mixed).astype(jnp.bfloat16)


def solution(mesh):
    finer = Mesh(
        mesh.devices.reshape(2, 8, mesh.shape["gy"], mesh.shape["gz"]), ("gx_0", "gx_1", "gy", "gz")
    )
    in_specs = (P(GX, ("gy", "gz"), None), P(GX, ("gy", "gz")), P(), P(), P(), P(), P(), P(), P())
    out_specs = P(GX, ("gy", "gz"), None)
    return jax.shard_map(
        on_device, mesh=finer, in_specs=in_specs, out_specs=out_specs, check_vma=False
    )
```

profile of v0, /device:TPU:1, one launch (start us, length us, event | category | flops | bytes accessed | tf_op | source)
XLA Modules:
  0.0 162.5 jit_solution(5244915075156663408)
XLA Ops:
  6.5 0.0 copy-start
  6.5 0.0 all-gather.4.cloned.1.call-start
  6.5 0.7 convert_element_type.32
  7.3 0.1 copy.54
  7.4 1.0 convert_reduce_fusion.1
  8.4 0.1 copy.50
  8.5 0.1 copy.51
  8.6 1.1 fusion.7
  9.7 0.1 copy.52
  9.8 0.1 copy.53
  9.9 0.0 copy-done
  9.9 1.3 fusion.21
  11.2 0.2 fusion.17
  11.3 11.9 %all-gather = bf16[64,16,128]{2,1,0:T(8,128)(2,1)} all-gather(bf16[32,16,128]{2,1,0:T(8,128)(2,1)S(1)} %get-tuple-element.6), channel_id=2, replica_groups=mesh['gx_0'=2,'gx_1'=8,'gy'=4,'gz'=8] {'gx_0'}, dimensions={0}, use_global_device_ids=true | all-gather | bytes 393216 | tf_op jit(solution)/shard_map/all_gather | solution.py:38
  23.3 0.0 all-gather.4.cloned.1.call-update
  23.3 1.1 broadcast_in_dim.2
  24.4 3.9 %all-to-all-start = ((bf16[4,64,16,128]{3,2,1,0:T(8,128)(2,1)}), bf16[4,64,16,128]{3,2,1,0:T(8,128)(2,1)S(1)}, u32[]{:S(2)}, u32[]{:S(2)}) async-start(bf16[4,64,16,128]{3,2,1,0:T(8,128)(2,1)} %broadcast_in_dim.2), calls=%async_computation | async-start | bytes 2097152 | tf_op jit(solution)/shard_map/all_to_all | solution.py:12
  28.3 41.2 %all-gather.4.cloned.1.call-done = bf16[16,32,16,128]{3,2,1,0:T(8,128)(2,1)} async-done(((bf16[2,32,16,128]{3,2,1,0:T(8,128)(2,1)}), bf16[16,32,16,128]{3,2,1,0:T(8,128)(2,1)}) %all-gather.4.cloned.1.call-update) | async-done | bytes 2097168 | tf_op jit(solution)/shard_map/all_gather | solution.py:38
  69.5 3.4 %copy.56 = bf16[2,8,32,16,128]{4,3,2,1,0:T(8,128)(2,1)} copy(bf16[2,8,32,16,128]{4,3,2,0,1:T(8,128)(2,1)} %bitcast.38) | data formatting | bytes 4194304 | tf_op jit(solution)/shard_map/transpose | solution.py:41
  72.9 0.0 all-to-all-done
  72.9 4.3 %all-to-all-start.1 = ((bf16[512,16,128]{2,1,0:T(8,128)(2,1)}), bf16[512,16,128]{2,1,0:T(8,128)(2,1)S(1)}, u32[]{:S(2)}, u32[]{:S(2)}) async-start(bf16[512,16,128]{2,1,0:T(8,128)(2,1)} %bitcast.7), calls=%async_computation.1 | async-start | bytes 4194304 | tf_op jit(solution)/shard_map/all_to_all | solution.py:89
  77.2 0.3 copy.64
  77.5 0.8 slice.28
  78.4 2.5 %copy.58 = bf16[32,64,128]{1,0,2:T(8,128)(2,1)S(1)} copy(bf16[32,64,128]{2,1,0:T(8,128)(2,1)} %bitcast.37) | data formatting | bytes 1048576 | tf_op jit(solution)/shard_map/slice | solution.py:30
  80.8 44.1 %all-to-all-done.1 = bf16[512,16,128]{2,1,0:T(8,128)(2,1)S(1)} async-done(((bf16[512,16,128]{2,1,0:T(8,128)(2,1)}), bf16[512,16,128]{2,1,0:T(8,128)(2,1)S(1)}, u32[]{:S(2)}, u32[]{:S(2)}) %all-to-all-start.1) | async-done | bytes 2097184 | tf_op jit(solution)/shard_map/all_to_all | solution.py:89
  125.0 3.8 %copy.57 = bf16[128,4,16,128]{0,2,1,3:T(8,128)(2,1)} copy(bf16[128,4,16,128]{3,2,0,1:T(8,128)(2,1)S(1)} %bitcast.34) | data formatting | bytes 4194304 | tf_op jit(solution)/shard_map/all_to_all | solution.py:89
  128.8 2.2 %fusion = bf16[128,32,128]{0,1,2:T(8,128)(2,1)S(1)} fusion(bf16[32,64,128]{1,0,2:T(8,128)(2,1)S(1)} %copy.58, bf16[128,64,128]{0,1,2:T(8,128)(2,1)} %bitcast.35), kind=kOutput, calls=%fused_computation.2 | convolution fusion | flops 67633152 | bytes 3670016 | tf_op jit(solution)/shard_map/jkc,ikc->jic/dot_general | solution.py:91
  131.1 0.0 copy-start.1
  131.1 0.0 copy-start.3
  131.1 0.0 copy-start.4
  131.1 0.0 copy-start.7
  131.1 2.3 %copy.59 = bf16[128,32,128]{2,1,0:T(8,128)(2,1)} copy(bf16[128,32,128]{0,1,2:T(8,128)(2,1)S(1)} %fusion) | data formatting | bytes 2097152 | tf_op jit(solution)/shard_map/convert_element_type | solution.py:91
  133.4 5.6 %all-to-all-start.2 = ((bf16[8,16,32,128]{3,2,1,0:T(8,128)(2,1)}), bf16[8,16,32,128]{3,2,1,0:T(8,128)(2,1)S(1)}, u32[]{:S(2)}, u32[]{:S(2)}) async-start(bf16[8,16,32,128]{3,2,1,0:T(8,128)(2,1)} %bitcast.12), calls=%async_computation.2 | async-start | bytes 2097152 | tf_op jit(solution)/shard_map/all_to_all | solution.py:56
  139.0 0.0 copy-done.1
  139.1 0.0 copy-done.4
  139.1 0.0 copy-done.7
  139.1 0.0 copy-start.5
  139.1 0.0 copy-start.6
  139.1 0.0 copy-start.2
  139.1 0.3 fusion.3
  139.5 14.6 %all-to-all-done.2 = bf16[8,16,32,128]{3,2,1,0:T(8,128)(2,1)S(1)} async-done(((bf16[8,16,32,128]{3,2,1,0:T(8,128)(2,1)}), bf16[8,16,32,128]{3,2,1,0:T(8,128)(2,1)S(1)}, u32[]{:S(2)}, u32[]{:S(2)}) %all-to-all-start.2) | async-done | bytes 1048608 | tf_op jit(solution)/shard_map/all_to_all | solution.py:56
  154.0 0.1 convert_reduce_fusion
  154.2 0.1 bitcast_reduce_fusion
  154.3 0.3 multiply_reduce_fusion
  154.6 0.0 copy-done.5
  154.6 0.0 copy-done.6
  154.6 0.2 add_convert_fusion
  154.8 0.8 fusion.4
  (7 shorter events, 0.1 us)
Async XLA Ops:
  6.5 3.3 %copy-start = (bf16[128,512]{1,0:T(8,128)(2,1)S(1)}, bf16[128,512]{1,0:T(8,128)(2,1)}, u32[]{:S(2)}) copy-start(bf16[128,512]{1,0:T(8,128)(2,1)} %param.13) | copy-start | bytes 393220
  6.5 63.0 %all-gather.4.cloned.1.call-start = ((), (), s32[]{:S(2)}) async-start(), calls=%async_computation.3 | async-start | bytes 2359296 | tf_op jit(solution)/shard_map/all_gather | solution.py:38
  24.4 48.4 %all-to-all-start = ((bf16[4,64,16,128]{3,2,1,0:T(8,128)(2,1)}), bf16[4,64,16,128]{3,2,1,0:T(8,128)(2,1)S(1)}, u32[]{:S(2)}, u32[]{:S(2)}) async-start(bf16[4,64,16,128]{3,2,1,0:T(8,128)(2,1)} %broadcast_in_dim.2), calls=%async_computation | async-start | bytes 2097152 | tf_op jit(solution)/shard_map/all_to_all | solution.py:12
  72.9 52.1 %all-to-all-start.1 = ((bf16[512,16,128]{2,1,0:T(8,128)(2,1)}), bf16[512,16,128]{2,1,0:T(8,128)(2,1)S(1)}, u32[]{:S(2)}, u32[]{:S(2)}) async-start(bf16[512,16,128]{2,1,0:T(8,128)(2,1)} %bitcast.7), calls=%async_computation.1 | async-start | bytes 4194304 | tf_op jit(solution)/shard_map/all_to_all | solution.py:89
  131.1 8.0 %copy-start.1 = (bf16[32,16,128]{2,1,0:T(8,128)(2,1)S(1)}, bf16[32,16,128]{2,1,0:T(8,128)(2,1)}, u32[]{:S(2)}) copy-start(bf16[32,16,128]{2,1,0:T(8,128)(2,1)} %param.9) | copy-start | bytes 393220
  131.1 8.0 %copy-start.3 = (f32[128]{0:T(128)S(1)}, f32[128]{0:T(128)}, u32[]{:S(2)}) copy-start(f32[128]{0:T(128)} %param.12) | copy-start | bytes 1540
  131.1 8.0 %copy-start.4 = (f32[128]{0:T(128)S(1)}, f32[128]{0:T(128)}, u32[]{:S(2)}) copy-start(f32[128]{0:T(128)} %param.11) | copy-start | bytes 1540
  131.1 8.0 %copy-start.7 = (bf16[128,128]{1,0:T(8,128)(2,1)S(1)}, bf16[128,128]{1,0:T(8,128)(2,1)}, u32[]{:S(2)}) copy-start(bf16[128,128]{1,0:T(8,128)(2,1)} %param.14) | copy-start | bytes 98308
  133.4 20.6 %all-to-all-start.2 = ((bf16[8,16,32,128]{3,2,1,0:T(8,128)(2,1)}), bf16[8,16,32,128]{3,2,1,0:T(8,128)(2,1)S(1)}, u32[]{:S(2)}, u32[]{:S(2)}) async-start(bf16[8,16,32,128]{3,2,1,0:T(8,128)(2,1)} %bitcast.12), calls=%async_computation.2 | async-start | bytes 2097152 | tf_op jit(solution)/shard_map/all_to_all | solution.py:56
  139.1 15.5 %copy-start.5 = (f32[128]{0:T(128)S(1)}, f32[128]{0:T(128)}, u32[]{:S(2)}) copy-start(f32[128]{0:T(128)} %param.16) | copy-start | bytes 1540
  139.1 15.5 %copy-start.6 = (f32[128]{0:T(128)S(1)}, f32[128]{0:T(128)}, u32[]{:S(2)}) copy-start(f32[128]{0:T(128)} %param.15) | copy-start | bytes 1540
  139.1 15.7 %copy-start.2 = (bf16[128,128]{1,0:T(8,128)(2,1)S(1)}, bf16[128,128]{1,0:T(8,128)(2,1)}, u32[]{:S(2)}) copy-start(bf16[128,128]{1,0:T(8,128)(2,1)} %param.17) | copy-start | bytes 98308
Sparse Core Ops, SparseCore 0:
  23.4 46.0 all-gather.3
where the time goes:
time: 163 us
  waiting for transfers between devices  99.9 us (61%)
  local copies, waits for them, and re-layouts  14.6 us (9%)
  starting transfers between devices  13.9 us (9%)
  between operations  13.6 us (8%)
  blocking collectives  11.9 us (7%)
  matrix products  4.71 us (3%)
  other arithmetic  3.89 us (2%)
    all_to_all x1, waiting for transfers between devices, on_device(): lax.all_to_all(every_row, 'gy', split_axis=0, concat_axis=1, tiled=True)  44.1 us
    all_gather x1, waiting for transfers between devices, stacked_from(): tiles = lax.all_gather(tiles, axes[k])  41.2 us
    all_to_all x1, waiting for transfers between devices, sent_and_summed(): tiles = lax.all_to_all(in_blocks(x, dim, size), axis, 0, 0, tiled=True)  14.6 us
    all_gather x1, blocking collectives, stacked_from(): tiles = lax.all_gather(tiles, axes[k])  11.9 us
    all_to_all x1, starting transfers between devices, sent_and_summed(): tiles = lax.all_to_all(in_blocks(x, dim, size), axis, 0, 0, tiled=True)  5.65 us
    all_to_all x1, starting transfers between devices, on_device(): lax.all_to_all(every_row, 'gy', split_axis=0, concat_axis=1, tiled=True)  4.31 us
    all_to_all x1, starting transfers between devices, sent_to_all(): return lax.all_to_all(copies, axis, split_axis=0, concat_axis=0, tiled=True)  3.91 us
    all_to_all x1, local copies, waits for them, and re-layouts, on_device(): lax.all_to_all(every_row, 'gy', split_axis=0, concat_axis=1, tiled=True)  3.84 us
  transfers between devices with their start and end apart: 4, of which 3 were waited for; matrix products, arithmetic and copies ran while one was open for 5% of the time, Pallas kernels for 0%

commit v1 on v0

v1 whole, which is shorter than its diff:
```python
import functools

import jax
import jax.numpy as jnp
from jax import lax
from jax.experimental import pallas as pl
from jax.experimental.pallas import tpu as pltpu
from jax.sharding import PartitionSpec as P

MESH = pl.DeviceIdType.MESH
F32, BF16 = jnp.float32, jnp.bfloat16
EPS = 1e-05


def dot(a, b, ca, cb):
    return lax.dot_general(a, b, (((ca,), (cb,)), ((), ())), preferred_element_type=F32)


def exchange_blocks(tiles):
    block = lax.broadcasted_iota(jnp.int32, tiles[0].shape, 1) // 32
    rolled = [[t if d == 0 else pltpu.roll(t, 32 * d, 1) for d in range(4)] for t in tiles]
    outs = []
    for b in range(4):
        out = rolled[0][(0 - b) % 4]
        for a in range(1, 4):
            out = jnp.where(block == a, rolled[a][(a - b) % 4], out)
        outs.append(out)
    return outs


def kernel(
    pair_hbm, mask_hbm, in_gain_hbm, in_bias_hbm, proj_hbm, gatew_hbm, out_gain_hbm, out_bias_hbm, outw_hbm,
    out_ref,
    pair, mask, in_gain, in_bias, proj, gatew, out_gain, out_bias, outw,
    normed, staged, send1, recv1, ops, oplane, xsend, xrecv, own, send3, tri, wide, gating, mixed,
    load_sem, s1, r1, sd, rd, sx, rx, s3, r3, se, re,
):
    gx, gy, gz = lax.axis_index("gx"), lax.axis_index("gy"), lax.axis_index("gz")
    x, core = gz // 2, gz % 2
    me = gx * 4 + gy
    partner = (gx, gy, x * 2 + 1 - core)

    def plane(p):
        return (p // 4, p % 4, gz)

    def along_x(d):
        return (gx, gy, ((x + d) % 4) * 2 + core)

    barrier = pltpu.get_barrier_semaphore()

    def greet(t, carry):
        pl.semaphore_signal(barrier, inc=1, device_id=plane((t + me) % 64), device_id_type=MESH)
        return carry

    lax.fori_loop(1, 64, greet, 0)
    for d in range(1, 4):
        pl.semaphore_signal(barrier, inc=1, device_id=along_x(d), device_id_type=MESH)
    pl.semaphore_signal(barrier, inc=1, device_id=partner, device_id_type=MESH)

    sources = (pair_hbm, mask_hbm, in_gain_hbm, in_bias_hbm, proj_hbm, gatew_hbm, out_gain_hbm, out_bias_hbm, outw_hbm)
    places = (pair, mask, in_gain, in_bias, proj, gatew, out_gain, out_bias, outw)
    loads = [pltpu.make_async_copy(s, d, load_sem.at[n]) for n, (s, d) in enumerate(zip(sources, places))]
    for load in loads:
        load.start()
    for load in loads:
        load.wait()

    tile = pair[...].astype(F32).reshape(512, 128)
    centered = tile - jnp.mean(tile, axis=-1, keepdims=True)
    variance = jnp.mean(centered * centered, axis=-1, keepdims=True)
    scaled = centered * lax.rsqrt(variance + EPS) * in_gain[...] + in_bias[...]
    normed[...] = scaled.astype(BF16).astype(F32)
    mask_value = mask[...].astype(F32)
    rows = []
    for k in range(16):
        rows.append(normed[pl.ds(k, 32, stride=16), :] * mask_value[:, k : k + 1])
    masked = jnp.concatenate(rows, axis=0).astype(BF16)
    projected = dot(jnp.transpose(proj[...]), masked, 1, 1)
    for side in range(2):
        gate = projected[256 * side : 256 * side + 128, :]
        value = projected[256 * side + 128 : 256 * side + 256, :]
        both = jax.nn.sigmoid(gate) * value
        for par in range(2):
            for q in range(4):
                staged[pl.ds(side * 8 + par * 4 + q, 64, stride=16), :] = both[
                    par * 64 : par * 64 + 64, q * 128 : q * 128 + 128
                ]
    send1[...] = staged[...].astype(BF16).reshape(64, 16, 128)

    pl.semaphore_wait(barrier, 67)

    def send_first(t, carry):
        p = (t + me) % 64
        pltpu.make_async_remote_copy(
            send1.at[p], recv1.at[me], s1, r1, device_id=plane(p), device_id_type=MESH
        ).start()
        return carry

    lax.fori_loop(1, 64, send_first, 0)
    recv1[me] = send1[me]

    gates = dot(normed[...].astype(BF16), gatew[...], 1, 0)
    gating[...] = jax.nn.sigmoid(gates).reshape(32, 16, 128)

    pltpu.make_async_copy(send1.at[pl.ds(0, 63)], send1.at[pl.ds(0, 63)], s1).wait()
    pltpu.make_async_copy(recv1.at[pl.ds(0, 63)], recv1.at[pl.ds(0, 63)], r1).wait()

    low = lax.broadcasted_iota(jnp.int32, (8, 128), 0) < 4
    for side in range(2):
        for group in range(4):
            for y in range(4):
                if side == 0:
                    members = [4 * group + a for a in range(4)]
                else:
                    members = [4 * a + group for a in range(4)]
                tiles = [recv1[m * 4 + y, side * 8 : side * 8 + 8, :].astype(F32) for m in members]
                outs = exchange_blocks(tiles)
                turned = [pltpu.roll(o, 4, 0) for o in outs]
                first = [jnp.where(low, outs[2 * h], turned[2 * h + 1]) for h in range(2)]
                second = [jnp.where(low, turned[2 * h], outs[2 * h + 1]) for h in range(2)]
                at = (pl.ds(y * 16, 16), pl.ds(group * 128, 128))
                ops[0, side, at[0], at[1]] = jnp.concatenate(first, axis=0).astype(BF16)
                ops[1, side, at[0], at[1]] = jnp.concatenate(second, axis=0).astype(BF16)

    cross = pltpu.make_async_remote_copy(
        ops.at[1 - core], oplane, sd, rd, device_id=partner, device_id_type=MESH
    )
    cross.start()
    left = [jnp.transpose(ops[core, 0])]
    cross.wait()
    left.append(jnp.transpose(oplane[0]))
    left = jnp.concatenate(left, axis=1)

    copies = []
    for d in range(1, 5):
        at = pl.ds(pl.multiple_of(((x + d) % 4) * 128, 128), 128)
        right = jnp.concatenate([ops[core, 1, :, at], oplane[1, :, at]], axis=0)
        part = dot(left, right, 1, 0)
        if d < 4:
            xsend[d - 1] = part.astype(BF16)
            copy = pltpu.make_async_remote_copy(
                xsend.at[d - 1], xrecv.at[d - 1], sx.at[d - 1], rx.at[d - 1], device_id=along_x(d), device_id_type=MESH
            )
            copy.start()
            copies.append(copy)
        else:
            own[...] = part
    for copy in copies:
        copy.wait()

    for g in range(16):
        tiles = []
        for s in range(4):
            at = pl.ds(g * 32 + s * 8, 8)
            total = own[at, :]
            for d in range(3):
                total = total + xrecv[d, at, :].astype(F32)
            tiles.append(total)
        for w, out in enumerate(exchange_blocks(tiles)):
            send3[g * 4 + w] = out.astype(BF16)

    def send_third(t, carry):
        p = (t + me) % 64
        pltpu.make_async_remote_copy(
            send3.at[p], tri.at[core, me], s3, r3, device_id=plane(p), device_id_type=MESH
        ).start()
        return carry

    lax.fori_loop(1, 64, send_third, 0)
    tri[core, me] = send3[me]
    pltpu.make_async_copy(send3.at[pl.ds(0, 63)], send3.at[pl.ds(0, 63)], s3).wait()
    pltpu.make_async_copy(send3.at[pl.ds(0, 63)], tri.at[core, pl.ds(0, 63)], r3).wait()
    swap = pltpu.make_async_remote_copy(
        tri.at[core], tri.at[core], se, re, device_id=partner, device_id_type=MESH
    )
    swap.start()
    gain = jnp.transpose(jnp.broadcast_to(out_gain[...], (128, 128)))
    bias = jnp.transpose(jnp.broadcast_to(out_bias[...], (128, 128)))
    swap.wait()

    wide[...] = tri[...].astype(F32).reshape(1024, 128)
    for r in range(8):
        sums = wide[pl.ds(r, 128, stride=8), :]
        off = sums - jnp.mean(sums, axis=0, keepdims=True)
        spread = jnp.mean(off * off, axis=0, keepdims=True)
        tri_normed = (off * lax.rsqrt(spread + EPS) * gain + bias).astype(BF16)
        mixed[r] = dot(jnp.transpose(tri_normed), outw[...], 1, 0).reshape(4, 2, 16, 128)
    for r in range(8):
        for s in range(4):
            out_ref[s * 8 + r] = (gating[s * 8 + r] * mixed[r, s, core]).astype(BF16)


def on_device(pair, pair_mask, in_gain, in_bias, proj_weight, gate_weight, out_gain, out_bias, out_weight):
    vmem = pltpu.VMEM
    dma = pltpu.SemaphoreType.DMA
    args = (
        pair, pair_mask, in_gain.reshape(1, 128), in_bias.reshape(1, 128), proj_weight, gate_weight,
        out_gain.reshape(1, 128), out_bias.reshape(1, 128), out_weight,
    )
    return pl.pallas_call(
        kernel,
        out_shape=jax.ShapeDtypeStruct((32, 16, 128), BF16),
        in_specs=[pl.BlockSpec(memory_space=pl.ANY)] * 9,
        out_specs=pl.BlockSpec(memory_space=pltpu.VMEM),
        scratch_shapes=[vmem(a.shape, a.dtype) for a in args]
        + [
            vmem((512, 128), F32),
            vmem((1024, 128), F32),
            vmem((64, 16, 128), BF16),
            vmem((64, 16, 128), BF16),
            vmem((2, 2, 64, 512), BF16),
            vmem((2, 64, 512), BF16),
            vmem((3, 512, 128), BF16),
            vmem((3, 512, 128), BF16),
            vmem((512, 128), F32),
            vmem((64, 8, 128), BF16),
            vmem((2, 64, 8, 128), BF16),
            vmem((1024, 128), F32),
            vmem((32, 16, 128), F32),
            vmem((8, 4, 2, 16, 128), F32),
            dma((9,)), dma, dma, dma, dma, dma((3,)), dma((3,)), dma, dma, dma, dma,
        ],
        compiler_params=pltpu.CompilerParams(collective_id=1, has_side_effects=True),
    )(*args)


def solution(mesh):
    rows = P("gx", ("gy", "gz"), None)
    in_specs = (rows, P("gx", ("gy", "gz")), P(), P(), P(), P(), P(), P(), P())
    return jax.shard_map(on_device, mesh=mesh, in_specs=in_specs, out_specs=rows, check_vma=False)
```

time: 163 us -> 51.8 us (0.32)
  waiting for transfers between devices: 99.9 us -> 0 us
  Pallas kernels: 0 us -> 48.6 us
  starting transfers between devices: 13.9 us -> 0 us
  between operations: 13.6 us -> 0.01 us
  blocking collectives: 11.9 us -> 0 us
  local copies, waits for them, and re-layouts: 14.6 us -> 2.94 us
  matrix products: 4.71 us -> 0 us
  other arithmetic: 3.89 us -> 0 us
    all_to_all x3 -> x0, waiting for transfers between devices: 58.7 us -> none  [the longest x1 44.1 us: on_device(): lax.all_to_all(every_row, 'gy', split_axis=0, concat_axis=1, tiled=True)]
    pallas_call x0 -> x1, Pallas kernels: none -> 48.6 us  [on_device(): pl.pallas_call(kernel, out_shape=jax.ShapeDtypeStruct((32, 16, 128), BF16...]
    all_gather x1 -> x0, waiting for transfers between devices: 41.2 us -> none  [stacked_from(): tiles = lax.all_gather(tiles, axes[k])]
    all_to_all x3 -> x0, starting transfers between devices: 13.9 us -> none  [the longest x1 5.65 us: sent_and_summed(): tiles = lax.all_to_all(in_blocks(x, dim, size), axis, 0, 0, tiled=True)]
    all_gather x1 -> x0, blocking collectives: 11.9 us -> none  [stacked_from(): tiles = lax.all_gather(tiles, axes[k])]
    dot_general x4 -> x0, matrix products: 4.71 us -> none  [the longest x1 2.25 us: on_device(): jnp.einsum('jkc,ikc->jic', row_panel, left_slab, preferred_element_type=j...]
    all_to_all x2 -> x0, local copies, waits for them, and re-layouts: 4.15 us -> none  [the longest x1 3.84 us: on_device(): lax.all_to_all(every_row, 'gy', split_axis=0, concat_axis=1, tiled=True)]
    transpose x1 -> x0, local copies, waits for them, and re-layouts: 3.37 us -> none  [stacked_from(): tiles = tiles.transpose(*back, *range(len(axes), tiles.ndim))]
  transfers between devices with their start and end apart: 4 -> 0, of which waited for: 3 -> 0; matrix products, arithmetic and copies ran while one was open for 5% -> 0% of each run, Pallas kernels for 0% -> 0%
where the time goes in v1:
time: 51.8 us; the launch traced here: 51.6 us
  Pallas kernels  48.6 us (94%)
  local copies, waits for them, and re-layouts  2.94 us (6%)
    pallas_call x1, Pallas kernels, on_device(): pl.pallas_call(kernel, out_shape=jax.ShapeDtypeStruct((32, 16, 128), BF16...  48.6 us
    unnamed x2, local copies, waits for them, and re-layouts  2.94 us

profile of v1, /device:TPU:1, one launch (start us, length us, event | category | flops | bytes accessed | tf_op | source)
XLA Modules:
  0.0 51.6 jit_solution(5332296566777205351)
XLA Ops:
  0.0 1.4 %copy.10.mask_hbm = s32[32,16]{1,0:T(8,128)} copy(s32[32,16]{0,1:T(8,128)} %param.10) | data formatting | bytes 4096 | tf_op args[1]
  1.4 48.6 %shard_map.91 = bf16[32,16,128]{2,1,0:T(8,128)(2,1)} custom-call(bf16[32,16,128]{2,1,0:T(8,128)(2,1)} %pair_hbm.1, s32[32,16]{1,0:T(8,128)} %copy.10.mask_hbm, f32[1,128]{1,0:T(1,128)} %bitcast.4, f32[1,128]{1,0:T(1,128)} %bitcast.5, bf16[128,512]{1,0:T(8,128)(2,1)} %proj_hbm.1, bf16[128,128]{1,0:T(8,128)(2,1)} %gatew_hbm.1, f32[1,128]{1,0:T(1,128)} %bitcast.6, ...), custom_call_target="tpu_custom_call" | custom-call | tf_op jit(solution)/shard_map/pallas_call | solution.py:200
  50.0 1.6 %copy.12 = bf16[32,16,128]{2,1,0:T(8,128)(2,1)} copy(bf16[32,16,128]{2,1,0:T(8,128)(2,1)} %shard_map.91) | data formatting | bytes 262144

commit v2 on v1

v2 whole, which is shorter than its diff:
```python
import jax
import jax.numpy as jnp
from jax import lax
from jax.experimental import pallas as pl
from jax.experimental.pallas import tpu as pltpu
from jax.sharding import PartitionSpec as P

MESH = pl.DeviceIdType.MESH
F32, BF16 = jnp.float32, jnp.bfloat16
EPS = 1e-05


def dot(a, b, ca, cb):
    return lax.dot_general(a, b, (((ca,), (cb,)), ((), ())), preferred_element_type=F32)


def lanes(shape):
    return lax.broadcasted_iota(jnp.int32, shape, 1)


def exchange_blocks(tiles):
    block = lanes(tiles[0].shape) // 32
    rolled = [[t if d == 0 else pltpu.roll(t, 32 * d, 1) for d in range(4)] for t in tiles]
    outs = []
    for b in range(4):
        out = rolled[0][(0 - b) % 4]
        for a in range(1, 4):
            out = jnp.where(block == a, rolled[a][(a - b) % 4], out)
        outs.append(out)
    return outs


def kernel(
    pair_hbm, mask_hbm, in_gain_hbm, in_bias_hbm, proj_hbm, gatew_hbm, out_gain_hbm, out_bias_hbm, outw_hbm,
    out_ref,
    pair, mask, in_gain, in_bias, proj, gatew, out_gain, out_bias, outw,
    normed, staged, send1, recv1, left, left_in, right, right_in, rows, xsend, xrecv, own, send3, tri, wide,
    gating, mixed,
    load_sem, s1, r1, sl, rl, sr, rr, sx, rx, s3, r3,
):
    gx, gy, gz = lax.axis_index("gx"), lax.axis_index("gy"), lax.axis_index("gz")
    x, core = gz // 2, gz % 2
    me = gx * 4 + gy
    partner = (gx, gy, x * 2 + 1 - core)

    def plane(p):
        return (p // 4, p % 4, gz)

    def along_x(d):
        return (gx, gy, ((x + d) % 4) * 2 + core)

    barrier = pltpu.get_barrier_semaphore()

    def greet(t, carry):
        pl.semaphore_signal(barrier, inc=1, device_id=plane((t + me) % 64), device_id_type=MESH)
        return carry

    lax.fori_loop(1, 64, greet, 0)
    for d in range(1, 4):
        pl.semaphore_signal(barrier, inc=1, device_id=along_x(d), device_id_type=MESH)
    pl.semaphore_signal(barrier, inc=1, device_id=partner, device_id_type=MESH)

    sources = (pair_hbm, mask_hbm, in_gain_hbm, in_bias_hbm, proj_hbm, gatew_hbm, out_gain_hbm, out_bias_hbm, outw_hbm)
    places = (pair, mask, in_gain, in_bias, proj, gatew, out_gain, out_bias, outw)
    loads = [pltpu.make_async_copy(s, d, load_sem.at[n]) for n, (s, d) in enumerate(zip(sources, places))]
    for load in loads:
        load.start()
    for load in loads:
        load.wait()

    tile = pair[...].astype(F32).reshape(512, 128)
    centered = tile - jnp.mean(tile, axis=-1, keepdims=True)
    variance = jnp.mean(centered * centered, axis=-1, keepdims=True)
    scaled = centered * lax.rsqrt(variance + EPS) * in_gain[...] + in_bias[...]
    normed[...] = scaled.astype(BF16).astype(F32)
    mask_value = jnp.transpose(mask[...].astype(F32))
    masked = []
    for k in range(16):
        masked.append(normed[pl.ds(k, 32, stride=16), :] * mask_value[:, k : k + 1])
    masked = jnp.concatenate(masked, axis=0).astype(BF16)
    projected = dot(jnp.transpose(proj[...]), masked, 1, 1)
    for side in range(2):
        gate = projected[256 * side : 256 * side + 128, :]
        value = projected[256 * side + 128 : 256 * side + 256, :]
        both = jax.nn.sigmoid(gate) * value
        for ch in range(2):
            for q in range(4):
                staged[ch, pl.ds(side * 4 + q, 64, stride=8), :] = both[
                    ch * 64 : ch * 64 + 64, q * 128 : q * 128 + 128
                ]
    for ch in range(2):
        send1[ch] = staged[ch].reshape(64, 8, 128).astype(BF16)

    pl.semaphore_wait(barrier, 67)

    for ch in range(2):

        def send_first(t, carry, ch=ch):
            p = (t + me) % 64
            pltpu.make_async_remote_copy(
                send1.at[ch, p], recv1.at[ch, me], s1.at[ch], r1.at[ch], device_id=plane(p), device_id_type=MESH
            ).start()
            return carry

        lax.fori_loop(1, 64, send_first, 0)
        recv1[ch, me] = send1[ch, me]

    gates = dot(normed[...].astype(BF16), gatew[...], 1, 0)
    gating[...] = jax.nn.sigmoid(gates)

    low = lax.broadcasted_iota(jnp.int32, (8, 128), 0) < 4
    near = lanes((8, 128)) % 32 < 16
    for ch in range(2):
        pltpu.make_async_copy(recv1.at[ch, pl.ds(0, 63)], recv1.at[ch, pl.ds(0, 63)], r1.at[ch]).wait()
        for pairing in range(2):
            at = [pl.ds(pairing * 32 + h * 16, 16) for h in range(2)]
            sides = [[], []]
            for g in range(16):
                one = recv1[ch, g * 4 + pairing * 2].astype(F32)
                two = recv1[ch, g * 4 + pairing * 2 + 1].astype(F32)
                sides[0].append(jnp.where(low, one, pltpu.roll(two, 4, 0)))
                sides[1].append(jnp.where(low, pltpu.roll(one, 4, 0), two))
            for group in range(4):
                outs = exchange_blocks([sides[0][4 * group + a] for a in range(4)])
                for h in range(2):
                    left[ch, at[h], pl.ds(group * 128, 128)] = jnp.concatenate(
                        [outs[2 * h], outs[2 * h + 1]], axis=0
                    ).astype(BF16)
            for xpair in range(2):
                both = [exchange_blocks([sides[1][4 * a + 2 * xpair + b] for a in range(4)]) for b in range(2)]
                for h in range(2):
                    halves = [[], []]
                    for kk in (2 * h, 2 * h + 1):
                        halves[0].append(jnp.where(near, both[0][kk], pltpu.roll(both[1][kk], 16, 1)))
                        halves[1].append(jnp.where(near, pltpu.roll(both[0][kk], 112, 1), both[1][kk]))
                    for c in range(2):
                        right[ch, c, at[h], pl.ds(xpair * 128, 128)] = jnp.concatenate(
                            halves[c], axis=0
                        ).astype(BF16)

        cross_left = pltpu.make_async_remote_copy(
            left.at[ch], left_in.at[ch], sl.at[ch], rl.at[ch], device_id=partner, device_id_type=MESH
        )
        cross_left.start()
        cross_right = pltpu.make_async_remote_copy(
            right.at[ch, 1 - core], right_in.at[ch], sr.at[ch], rr.at[ch], device_id=partner, device_id_type=MESH
        )
        cross_right.start()
        cross_left.wait()
        cross_right.wait()
        both = jnp.concatenate([right[ch, core], right_in[ch]], axis=0)
        turned = jnp.transpose(both)
        for xx in range(4):
            for v in range(4):
                at = ((xx // 2 * 4 + v) * 2 + xx % 2) * 16
                rows[xx, v * 16 : v * 16 + 16, :] = turned[at : at + 16, :]
        stacked = jnp.concatenate([left[ch], left_in[ch]], axis=0)
        for d in (2, 1, 3, 4):
            part = dot(rows[(x + d) % 4], stacked, 1, 0)
            for q in range(4):
                if d < 4:
                    xsend[ch, d - 1, q] = part[:, q * 128 : q * 128 + 128].astype(BF16)
                else:
                    own[ch, q] = part[:, q * 128 : q * 128 + 128]
            if d < 4:
                for t in range(4):
                    q = (gx // 4 + 3 - t) % 4
                    pltpu.make_async_remote_copy(
                        xsend.at[ch, d - 1, q], xrecv.at[ch, d - 1, q], sx.at[ch, d - 1, t], rx.at[ch, d - 1, t],
                        device_id=along_x(d), device_id_type=MESH,
                    ).start()

    for t in range(4):
        q = (gx // 4 + 3 - t) % 4
        totals = []
        for ch in range(2):
            for d in range(3):
                pltpu.make_async_copy(xrecv.at[ch, d, q], xrecv.at[ch, d, q], rx.at[ch, d, t]).wait()
            total = own[ch, q]
            for d in range(3):
                total = total + xrecv[ch, d, q].astype(F32)
            totals.append(total)
        for v in range(4):
            tiles = [totals[ch][v * 16 + s * 8 : v * 16 + s * 8 + 8, :] for ch in range(2) for s in range(2)]
            for g, out in enumerate(exchange_blocks(tiles)):
                send3[q, g * 4 + v] = out.astype(BF16)

        def send_third(n, carry, q=q):
            p = q * 16 + n

            @pl.when(p != me)
            def _():
                pltpu.make_async_remote_copy(
                    send3.at[q, n], tri.at[me], s3, r3, device_id=plane(p), device_id_type=MESH
                ).start()

            return carry

        lax.fori_loop(0, 16, send_third, 0)
    tri[me] = send3[gx // 4, me % 16]

    gain = jnp.transpose(jnp.broadcast_to(out_gain[...], (128, 128)))
    bias = jnp.transpose(jnp.broadcast_to(out_bias[...], (128, 128)))
    for ch in range(2):
        pltpu.make_async_copy(send1.at[ch, pl.ds(0, 63)], send1.at[ch, pl.ds(0, 63)], s1.at[ch]).wait()
        for d in range(3):
            for t in range(4):
                pltpu.make_async_copy(xsend.at[ch, d, t], xsend.at[ch, d, t], sx.at[ch, d, t]).wait()
    pltpu.make_async_copy(tri.at[pl.ds(0, 63)], tri.at[pl.ds(0, 63)], r3).wait()

    wide[...] = tri[...].astype(F32).reshape(512, 128)
    first = lanes((64, 128)) < 64
    for m in range(4):
        one = wide[pl.ds(2 * m, 64, stride=8), :]
        two = wide[pl.ds(2 * m + 1, 64, stride=8), :]
        sums = jnp.concatenate(
            [jnp.where(first, one, pltpu.roll(two, 64, 1)), jnp.where(first, pltpu.roll(one, 64, 1), two)], axis=0
        )
        off = sums - jnp.mean(sums, axis=0, keepdims=True)
        spread = jnp.mean(off * off, axis=0, keepdims=True)
        tri_normed = (off * lax.rsqrt(spread + EPS) * gain + bias).astype(BF16)
        result = dot(jnp.transpose(tri_normed), outw[...], 1, 0)
        for r in range(2):
            for s in range(2):
                at = (r * 2 + s) * 32
                mixed[pl.ds(s * 8 + 2 * m + r, 32, stride=16), :] = result[at : at + 32, :]
    out_ref[...] = (gating[...] * mixed[...]).astype(BF16).reshape(32, 16, 128)
    pltpu.make_async_copy(tri.at[pl.ds(0, 63)], tri.at[pl.ds(0, 63)], s3).wait()


def on_device(pair, pair_mask, in_gain, in_bias, proj_weight, gate_weight, out_gain, out_bias, out_weight):
    vmem = pltpu.VMEM
    dma = pltpu.SemaphoreType.DMA
    args = (
        pair, pair_mask.T, in_gain.reshape(1, 128), in_bias.reshape(1, 128), proj_weight, gate_weight,
        out_gain.reshape(1, 128), out_bias.reshape(1, 128), out_weight,
    )
    return pl.pallas_call(
        kernel,
        out_shape=jax.ShapeDtypeStruct((32, 16, 128), BF16),
        in_specs=[pl.BlockSpec(memory_space=pl.ANY)] * 9,
        out_specs=pl.BlockSpec(memory_space=pltpu.VMEM),
        scratch_shapes=[vmem(a.shape, a.dtype) for a in args]
        + [
            vmem((512, 128), F32),
            vmem((2, 512, 128), F32),
            vmem((2, 64, 8, 128), BF16),
            vmem((2, 64, 8, 128), BF16),
            vmem((2, 64, 512), BF16),
            vmem((2, 64, 512), BF16),
            vmem((2, 2, 64, 256), BF16),
            vmem((2, 64, 256), BF16),
            vmem((4, 64, 128), BF16),
            vmem((2, 3, 4, 64, 128), BF16),
            vmem((2, 3, 4, 64, 128), BF16),
            vmem((2, 4, 64, 128), F32),
            vmem((4, 16, 8, 128), BF16),
            vmem((64, 8, 128), BF16),
            vmem((512, 128), F32),
            vmem((512, 128), F32),
            vmem((512, 128), F32),
            dma((9,)), dma((2,)), dma((2,)), dma((2,)), dma((2,)), dma((2,)), dma((2,)),
            dma((2, 3, 4)), dma((2, 3, 4)), dma, dma,
        ],
        compiler_params=pltpu.CompilerParams(collective_id=1, has_side_effects=True),
    )(*args)


def solution(mesh):
    rows = P("gx", ("gy", "gz"), None)
    in_specs = (rows, P("gx", ("gy", "gz")), P(), P(), P(), P(), P(), P(), P())
    return jax.shard_map(on_device, mesh=mesh, in_specs=in_specs, out_specs=rows, check_vma=False)
```

time: 51.8 us -> 46.5 us (0.90)
  Pallas kernels: 48.6 us -> 44.8 us
  local copies, waits for them, and re-layouts: 2.94 us -> 1.57 us
    pallas_call x1, Pallas kernels: 48.6 us -> 44.8 us  [on_device(): pl.pallas_call(kernel, out_shape=jax.ShapeDtypeStruct((32, 16, 128), BF16...]
    unnamed x2 -> x1, local copies, waits for them, and re-layouts: 2.94 us -> 1.57 us
where the time goes in v2:
time: 46.5 us; the launch traced here: 46.4 us
  Pallas kernels  44.8 us (96%)
  local copies, waits for them, and re-layouts  1.57 us (3%)
    pallas_call x1, Pallas kernels, on_device(): pl.pallas_call(kernel, out_shape=jax.ShapeDtypeStruct((32, 16, 128), BF16...  44.8 us
    unnamed x1, local copies, waits for them, and re-layouts  1.57 us

profile of v2, /device:TPU:1, one launch (start us, length us, event | category | flops | bytes accessed | tf_op | source)
XLA Modules:
  0.0 46.4 jit_solution(7466501134824079515)
XLA Ops:
  0.0 44.8 %shard_map.91 = bf16[32,16,128]{2,1,0:T(8,128)(2,1)} custom-call(bf16[32,16,128]{2,1,0:T(8,128)(2,1)} %pair_hbm.1, s32[16,32]{1,0:T(8,128)} %bitcast.5, f32[1,128]{1,0:T(1,128)} %bitcast.6, f32[1,128]{1,0:T(1,128)} %bitcast.7, bf16[128,512]{1,0:T(8,128)(2,1)} %proj_hbm.1, bf16[128,128]{1,0:T(8,128)(2,1)} %gatew_hbm.1, f32[1,128]{1,0:T(1,128)} %bitcast.8, ...), custom_call_target="tpu_custom_call" | custom-call | tf_op jit(solution)/shard_map/pallas_call | solution.py:238
  44.8 1.6 %copy.11 = bf16[32,16,128]{2,1,0:T(8,128)(2,1)} copy(bf16[32,16,128]{2,1,0:T(8,128)(2,1)} %shard_map.91) | data formatting | bytes 262144

commit v3 on v2

--- a/solution.py
+++ b/solution.py
@@ -8,6 +8,18 @@
 MESH = pl.DeviceIdType.MESH
 F32, BF16 = jnp.float32, jnp.bfloat16
 EPS = 1e-05
+
+
+CHUNKS = (0, 2, 1, 3)
+
+
+def around(d):
+    return min(d, 8 - d)
+
+
+STEPS = sorted(
+    [(a, b) for a in range(8) for b in range(8) if a or b], key=lambda s: -around(s[0]) - around(s[1])
+)
 
 
 def dot(a, b, ca, cb):
@@ -43,19 +55,23 @@
     me = gx * 4 + gy
     partner = (gx, gy, x * 2 + 1 - core)
 
+    y = gx // 8 * 4 + gy
+    zs = [(gx + d) % 8 for d in range(8)]
+    ys = [(y + d) % 8 for d in range(8)]
+    tops, lows = [v // 4 * 8 for v in ys], [v % 4 for v in ys]
+
     def plane(p):
         return (p // 4, p % 4, gz)
 
+    others = [(tops[b] + zs[a], lows[b]) for a, b in STEPS]
+
     def along_x(d):
         return (gx, gy, ((x + d) % 4) * 2 + core)
 
     barrier = pltpu.get_barrier_semaphore()
 
-    def greet(t, carry):
-        pl.semaphore_signal(barrier, inc=1, device_id=plane((t + me) % 64), device_id_type=MESH)
-        return carry
-
-    lax.fori_loop(1, 64, greet, 0)
+    for g, w in others:
+        pl.semaphore_signal(barrier, inc=1, device_id=(g, w, gz), device_id_type=MESH)
     for d in range(1, 4):
         pl.semaphore_signal(barrier, inc=1, device_id=along_x(d), device_id_type=MESH)
     pl.semaphore_signal(barrier, inc=1, device_id=partner, device_id_type=MESH)
@@ -94,15 +110,11 @@
     pl.semaphore_wait(barrier, 67)
 
     for ch in range(2):
-
-        def send_first(t, carry, ch=ch):
-            p = (t + me) % 64
+        for g, w in others:
             pltpu.make_async_remote_copy(
-                send1.at[ch, p], recv1.at[ch, me], s1.at[ch], r1.at[ch], device_id=plane(p), device_id_type=MESH
+                send1.at[ch, g * 4 + w], recv1.at[ch, me], s1.at[ch], r1.at[ch], device_id=(g, w, gz),
+                device_id_type=MESH,
             ).start()
-            return carry
-
-        lax.fori_loop(1, 64, send_first, 0)
         recv1[ch, me] = send1[ch, me]
 
     gates = dot(normed[...].astype(BF16), gatew[...], 1, 0)
@@ -163,15 +175,13 @@
                 else:
                     own[ch, q] = part[:, q * 128 : q * 128 + 128]
             if d < 4:
-                for t in range(4):
-                    q = (gx // 4 + 3 - t) % 4
+                for t, q in enumerate(CHUNKS):
                     pltpu.make_async_remote_copy(
                         xsend.at[ch, d - 1, q], xrecv.at[ch, d - 1, q], sx.at[ch, d - 1, t], rx.at[ch, d - 1, t],
                         device_id=along_x(d), device_id_type=MESH,
                     ).start()
 
-    for t in range(4):
-        q = (gx // 4 + 3 - t) % 4
+    for t, q in enumerate(CHUNKS):
         totals = []
         for ch in range(2):
             for d in range(3):
@@ -185,18 +195,15 @@
             for g, out in enumerate(exchange_blocks(tiles)):
                 send3[q, g * 4 + v] = out.astype(BF16)
 
-        def send_third(n, carry, q=q):
+        for n in range(16):
             p = q * 16 + n
 
             @pl.when(p != me)
-            def _():
+            def _(n=n, p=p):
                 pltpu.make_async_remote_copy(
                     send3.at[q, n], tri.at[me], s3, r3, device_id=plane(p), device_id_type=MESH
                 ).start()
 
-            return carry
-
-        lax.fori_loop(0, 16, send_third, 0)
     tri[me] = send3[gx // 4, me % 16]
 
     gain = jnp.transpose(jnp.broadcast_to(out_gain[...], (128, 128)))
@@ -210,19 +217,25 @@
 
     wide[...] = tri[...].astype(F32).reshape(512, 128)
     first = lanes((64, 128)) < 64
+    pieces = []
     for m in range(4):
         one = wide[pl.ds(2 * m, 64, stride=8), :]
         two = wide[pl.ds(2 * m + 1, 64, stride=8), :]
-        sums = jnp.concatenate(
-            [jnp.where(first, one, pltpu.roll(two, 64, 1)), jnp.where(first, pltpu.roll(one, 64, 1), two)], axis=0
+        pieces.append(
+            jnp.concatenate(
+                [jnp.where(first, one, pltpu.roll(two, 64, 1)), jnp.where(first, pltpu.roll(one, 64, 1), two)], axis=0
+            )
         )
-        off = sums - jnp.mean(sums, axis=0, keepdims=True)
-        spread = jnp.mean(off * off, axis=0, keepdims=True)
-        tri_normed = (off * lax.rsqrt(spread + EPS) * gain + bias).astype(BF16)
-        result = dot(jnp.transpose(tri_normed), outw[...], 1, 0)
+    sums = jnp.concatenate(pieces, axis=1)
+    off = sums - jnp.mean(sums, axis=0, keepdims=True)
+    spread = jnp.mean(off * off, axis=0, keepdims=True)
+    scaled = off * lax.rsqrt(spread + EPS)
+    tri_normed = jnp.concatenate([scaled[:, m * 128 : m * 128 + 128] * gain + bias for m in range(4)], axis=1)
+    result = dot(jnp.transpose(tri_normed.astype(BF16)), outw[...], 1, 0)
+    for m in range(4):
         for r in range(2):
             for s in range(2):
-                at = (r * 2 + s) * 32
+                at = m * 128 + (r * 2 + s) * 32
                 mixed[pl.ds(s * 8 + 2 * m + r, 32, stride=16), :] = result[at : at + 32, :]
     out_ref[...] = (gating[...] * mixed[...]).astype(BF16).reshape(32, 16, 128)
     pltpu.make_async_copy(tri.at[pl.ds(0, 63)], tri.at[pl.ds(0, 63)], s3).wait()
@@ -238,7 +251,7 @@
     return pl.pallas_call(
         kernel,
         out_shape=jax.ShapeDtypeStruct((32, 16, 128), BF16),
-        in_specs=[pl.BlockSpec(memory_space=pl.ANY)] * 9,
+        in_specs=[pl.BlockSpec(memory_space=pltpu.HBM)] * 9,
         out_specs=pl.BlockSpec(memory_space=pltpu.VMEM),
         scratch_shapes=[vmem(a.shape, a.dtype) for a in args]
         + [

time: 46.5 us -> 43.5 us (0.935)
  Pallas kernels: 44.8 us -> 41.8 us
    pallas_call x1, Pallas kernels: 44.8 us -> 41.8 us  [on_device(): pl.pallas_call(kernel, out_shape=jax.ShapeDtypeStruct((32, 16, 128), BF16...]
where the time goes in v3:
time: 43.5 us; the launch traced here: 43.4 us
  Pallas kernels  41.8 us (96%)
  local copies, waits for them, and re-layouts  1.57 us (4%)
    pallas_call x1, Pallas kernels, on_device(): pl.pallas_call(kernel, out_shape=jax.ShapeDtypeStruct((32, 16, 128), BF16...  41.8 us
    unnamed x1, local copies, waits for them, and re-layouts  1.57 us

profile of v3, /device:TPU:1, one launch (start us, length us, event | category | flops | bytes accessed | tf_op | source)
XLA Modules:
  0.0 43.4 jit_solution(15450834982593576334)
XLA Ops:
  0.0 41.8 %shard_map.91 = bf16[32,16,128]{2,1,0:T(8,128)(2,1)} custom-call(bf16[32,16,128]{2,1,0:T(8,128)(2,1)} %pair_hbm.1, s32[16,32]{1,0:T(8,128)} %bitcast.5, f32[1,128]{1,0:T(1,128)} %bitcast.6, f32[1,128]{1,0:T(1,128)} %bitcast.7, bf16[128,512]{1,0:T(8,128)(2,1)} %proj_hbm.1, bf16[128,128]{1,0:T(8,128)(2,1)} %gatew_hbm.1, f32[1,128]{1,0:T(1,128)} %bitcast.8, ...), custom_call_target="tpu_custom_call" | custom-call | tf_op jit(solution)/shard_map/pallas_call | solution.py:251
  41.8 1.6 %copy.11 = bf16[32,16,128]{2,1,0:T(8,128)(2,1)} copy(bf16[32,16,128]{2,1,0:T(8,128)(2,1)} %shard_map.91) | data formatting | bytes 262144

commit v4 on v3

--- a/solution.py
+++ b/solution.py
@@ -248,9 +248,10 @@
         pair, pair_mask.T, in_gain.reshape(1, 128), in_bias.reshape(1, 128), proj_weight, gate_weight,
         out_gain.reshape(1, 128), out_bias.reshape(1, 128), out_weight,
     )
+    args = tuple(pltpu.with_memory_space_constraint(a, pltpu.HBM) for a in args)
     return pl.pallas_call(
         kernel,
-        out_shape=jax.ShapeDtypeStruct((32, 16, 128), BF16),
+        out_shape=pltpu.VMEM((32, 16, 128), BF16),
         in_specs=[pl.BlockSpec(memory_space=pltpu.HBM)] * 9,
         out_specs=pl.BlockSpec(memory_space=pltpu.VMEM),
         scratch_shapes=[vmem(a.shape, a.dtype) for a in args]

time: 43.5 us -> 42 us (0.966)
  local copies, waits for them, and re-layouts: 1.57 us -> 0.66 us
  Pallas kernels: 41.8 us -> 41.2 us
    unnamed x1, local copies, waits for them, and re-layouts: 1.57 us -> 0.66 us
    pallas_call x1, Pallas kernels: 41.8 us -> 41.2 us  [on_device(): pl.pallas_call(kernel, out_shape=pltpu.VMEM((32, 16, 128), BF16), in_spec...]
where the time goes in v4:
time: 42 us; the launch traced here: 41.8 us
  Pallas kernels  41.2 us (98%)
  local copies, waits for them, and re-layouts  0.66 us (2%)
    pallas_call x1, Pallas kernels, on_device(): pl.pallas_call(kernel, out_shape=pltpu.VMEM((32, 16, 128), BF16), in_spec...  41.2 us

profile of v4, /device:TPU:1, one launch (start us, length us, event | category | flops | bytes accessed | tf_op | source)
XLA Modules:
  0.0 41.8 jit_solution(10088721561958988133)
XLA Ops:
  0.0 41.2 %shard_map.91 = bf16[32,16,128]{2,1,0:T(8,128)(2,1)S(1)} custom-call(bf16[32,16,128]{2,1,0:T(8,128)(2,1)} %pair_hbm.1, s32[16,32]{1,0:T(8,128)} %bitcast.5, f32[1,128]{1,0:T(1,128)} %bitcast.6, f32[1,128]{1,0:T(1,128)} %bitcast.7, bf16[128,512]{1,0:T(8,128)(2,1)} %proj_hbm.1, bf16[128,128]{1,0:T(8,128)(2,1)} %gatew_hbm.1, f32[1,128]{1,0:T(1,128)} %bitcast.8, ...), custom_call_target="tpu_custom_call" | custom-call | tf_op jit(solution)/shard_map/pallas_call | solution.py:252
  41.2 0.7 %copy.11 = bf16[32,16,128]{2,1,0:T(8,128)(2,1)} copy(bf16[32,16,128]{2,1,0:T(8,128)(2,1)S(1)} %shard_map.91) | data formatting | bytes 262144

commit v5 on v4

--- a/solution.py
+++ b/solution.py
@@ -8,9 +8,6 @@
 MESH = pl.DeviceIdType.MESH
 F32, BF16 = jnp.float32, jnp.bfloat16
 EPS = 1e-05
-
-
-CHUNKS = (0, 2, 1, 3)
 
 
 def around(d):
@@ -110,6 +107,12 @@
     pl.semaphore_wait(barrier, 67)
 
     for ch in range(2):
+        if ch == 1:
+
+            @pl.when(core == 1)
+            def _():
+                pl.delay(2500)
+
         for g, w in others:
             pltpu.make_async_remote_copy(
                 send1.at[ch, g * 4 + w], recv1.at[ch, me], s1.at[ch], r1.at[ch], device_id=(g, w, gz),
@@ -122,6 +125,21 @@
 
     low = lax.broadcasted_iota(jnp.int32, (8, 128), 0) < 4
     near = lanes((8, 128)) % 32 < 16
+    def partial_sums(ch, wave):
+        both = jnp.concatenate([left[ch, wave], left_in[ch, wave]], axis=0)
+        part = dot(rows[ch], both, 1, 0)
+        for xx in range(4):
+            for top in range(2):
+                piece = part[xx * 64 : xx * 64 + 64, top * 128 : top * 128 + 128]
+                own[ch, wave, xx, top] = piece
+                xsend[ch, wave, xx, top] = piece.astype(BF16)
+
+    def send_along_x(ch, wave, d):
+        pltpu.make_async_remote_copy(
+            xsend.at[ch, wave, (x + d) % 4], xrecv.at[ch, wave, d - 1], sx.at[ch, wave, d - 1], rx.at[ch, wave, d - 1],
+            device_id=along_x(d), device_id_type=MESH,
+        ).start()
+
     for ch in range(2):
         pltpu.make_async_copy(recv1.at[ch, pl.ds(0, 63)], recv1.at[ch, pl.ds(0, 63)], r1.at[ch]).wait()
         for pairing in range(2):
@@ -135,7 +153,7 @@
             for group in range(4):
                 outs = exchange_blocks([sides[0][4 * group + a] for a in range(4)])
                 for h in range(2):
-                    left[ch, at[h], pl.ds(group * 128, 128)] = jnp.concatenate(
+                    left[ch, group % 2, at[h], pl.ds(group // 2 * 128, 128)] = jnp.concatenate(
                         [outs[2 * h], outs[2 * h + 1]], axis=0
                     ).astype(BF16)
             for xpair in range(2):
@@ -158,51 +176,51 @@
             right.at[ch, 1 - core], right_in.at[ch], sr.at[ch], rr.at[ch], device_id=partner, device_id_type=MESH
         )
         cross_right.start()
+        if ch == 1:
+            partial_sums(0, 1)
         cross_left.wait()
         cross_right.wait()
-        both = jnp.concatenate([right[ch, core], right_in[ch]], axis=0)
-        turned = jnp.transpose(both)
+        turned = jnp.transpose(jnp.concatenate([right[ch, core], right_in[ch]], axis=0))
         for xx in range(4):
             for v in range(4):
                 at = ((xx // 2 * 4 + v) * 2 + xx % 2) * 16
-                rows[xx, v * 16 : v * 16 + 16, :] = turned[at : at + 16, :]
-        stacked = jnp.concatenate([left[ch], left_in[ch]], axis=0)
-        for d in (2, 1, 3, 4):
-            part = dot(rows[(x + d) % 4], stacked, 1, 0)
-            for q in range(4):
-                if d < 4:
-                    xsend[ch, d - 1, q] = part[:, q * 128 : q * 128 + 128].astype(BF16)
-                else:
-                    own[ch, q] = part[:, q * 128 : q * 128 + 128]
-            if d < 4:
-                for t, q in enumerate(CHUNKS):
-                    pltpu.make_async_remote_copy(
-                        xsend.at[ch, d - 1, q], xrecv.at[ch, d - 1, q], sx.at[ch, d - 1, t], rx.at[ch, d - 1, t],
-                        device_id=along_x(d), device_id_type=MESH,
-                    ).start()
-
-    for t, q in enumerate(CHUNKS):
-        totals = []
+                rows[ch, xx * 64 + v * 16 : xx * 64 + v * 16 + 16, :] = turned[at : at + 16, :]
+        partial_sums(ch, 0)
+        for d in (2, 1, 3):
+            send_along_x(ch, 0, d)
+    partial_sums(1, 1)
+    for ch in range(2):
+        for d in range(3):
+            pltpu.make_async_copy(xsend.at[ch, 0, d], xsend.at[ch, 0, d], sx.at[ch, 0, d]).wait()
+    for ch in range(2):
+        for d in (2, 1, 3):
+            send_along_x(ch, 1, d)
+
+    for wave in range(2):
         for ch in range(2):
             for d in range(3):
-                pltpu.make_async_copy(xrecv.at[ch, d, q], xrecv.at[ch, d, q], rx.at[ch, d, t]).wait()
-            total = own[ch, q]
-            for d in range(3):
-                total = total + xrecv[ch, d, q].astype(F32)
-            totals.append(total)
-        for v in range(4):
-            tiles = [totals[ch][v * 16 + s * 8 : v * 16 + s * 8 + 8, :] for ch in range(2) for s in range(2)]
-            for g, out in enumerate(exchange_blocks(tiles)):
-                send3[q, g * 4 + v] = out.astype(BF16)
-
-        for n in range(16):
-            p = q * 16 + n
-
-            @pl.when(p != me)
-            def _(n=n, p=p):
-                pltpu.make_async_remote_copy(
-                    send3.at[q, n], tri.at[me], s3, r3, device_id=plane(p), device_id_type=MESH
-                ).start()
+                pltpu.make_async_copy(xrecv.at[ch, wave, d], xrecv.at[ch, wave, d], rx.at[ch, wave, d]).wait()
+        for top in range(2):
+            q = top * 2 + wave
+            totals = []
+            for ch in range(2):
+                total = own[ch, wave, x, top]
+                for d in range(3):
+                    total = total + xrecv[ch, wave, d, top].astype(F32)
+                totals.append(total)
+            for v in range(4):
+                tiles = [totals[ch][v * 16 + s * 8 : v * 16 + s * 8 + 8, :] for ch in range(2) for s in range(2)]
+                for g, out in enumerate(exchange_blocks(tiles)):
+                    send3[q, g * 4 + v] = out.astype(BF16)
+
+            for n in range(16):
+                p = q * 16 + n
+
+                @pl.when(p != me)
+                def _(n=n, p=p, q=q):
+                    pltpu.make_async_remote_copy(
+                        send3.at[q, n], tri.at[me], s3, r3, device_id=plane(p), device_id_type=MESH
+                    ).start()
 
     tri[me] = send3[gx // 4, me % 16]
 
@@ -211,8 +229,7 @@
     for ch in range(2):
         pltpu.make_async_copy(send1.at[ch, pl.ds(0, 63)], send1.at[ch, pl.ds(0, 63)], s1.at[ch]).wait()
         for d in range(3):
-            for t in range(4):
-                pltpu.make_async_copy(xsend.at[ch, d, t], xsend.at[ch, d, t], sx.at[ch, d, t]).wait()
+            pltpu.make_async_copy(xsend.at[ch, 1, d], xsend.at[ch, 1, d], sx.at[ch, 1, d]).wait()
     pltpu.make_async_copy(tri.at[pl.ds(0, 63)], tri.at[pl.ds(0, 63)], r3).wait()
 
     wide[...] = tri[...].astype(F32).reshape(512, 128)
@@ -260,21 +277,21 @@
             vmem((2, 512, 128), F32),
             vmem((2, 64, 8, 128), BF16),
             vmem((2, 64, 8, 128), BF16),
-            vmem((2, 64, 512), BF16),
-            vmem((2, 64, 512), BF16),
+            vmem((2, 2, 64, 256), BF16),
+            vmem((2, 2, 64, 256), BF16),
             vmem((2, 2, 64, 256), BF16),
             vmem((2, 64, 256), BF16),
-            vmem((4, 64, 128), BF16),
-            vmem((2, 3, 4, 64, 128), BF16),
-            vmem((2, 3, 4, 64, 128), BF16),
-            vmem((2, 4, 64, 128), F32),
+            vmem((2, 256, 128), BF16),
+            vmem((2, 2, 4, 2, 64, 128), BF16),
+            vmem((2, 2, 3, 2, 64, 128), BF16),
+            vmem((2, 2, 4, 2, 64, 128), F32),
             vmem((4, 16, 8, 128), BF16),
             vmem((64, 8, 128), BF16),
             vmem((512, 128), F32),
             vmem((512, 128), F32),
             vmem((512, 128), F32),
             dma((9,)), dma((2,)), dma((2,)), dma((2,)), dma((2,)), dma((2,)), dma((2,)),
-            dma((2, 3, 4)), dma((2, 3, 4)), dma, dma,
+            dma((2, 2, 3)), dma((2, 2, 3)), dma, dma,
         ],
         compiler_params=pltpu.CompilerParams(collective_id=1, has_side_effects=True),
     )(*args)

time: 42 us -> 39.8 us (0.948)
  Pallas kernels: 41.2 us -> 39 us
    pallas_call x1, Pallas kernels: 41.2 us -> 39 us  [on_device(): pl.pallas_call(kernel, out_shape=pltpu.VMEM((32, 16, 128), BF16), in_spec...]
where the time goes in v5:
time: 39.8 us; the launch traced here: 39.6 us
  Pallas kernels  39 us (98%)
  local copies, waits for them, and re-layouts  0.66 us (2%)
    pallas_call x1, Pallas kernels, on_device(): pl.pallas_call(kernel, out_shape=pltpu.VMEM((32, 16, 128), BF16), in_spec...  39 us

profile of v5, /device:TPU:1, one launch (start us, length us, event | category | flops | bytes accessed | tf_op | source)
XLA Modules:
  0.0 39.6 jit_solution(5215682790119480904)
XLA Ops:
  0.0 39.0 %shard_map.91 = bf16[32,16,128]{2,1,0:T(8,128)(2,1)S(1)} custom-call(bf16[32,16,128]{2,1,0:T(8,128)(2,1)} %pair_hbm.1, s32[16,32]{1,0:T(8,128)} %bitcast.5, f32[1,128]{1,0:T(1,128)} %bitcast.6, f32[1,128]{1,0:T(1,128)} %bitcast.7, bf16[128,512]{1,0:T(8,128)(2,1)} %proj_hbm.1, bf16[128,128]{1,0:T(8,128)(2,1)} %gatew_hbm.1, f32[1,128]{1,0:T(1,128)} %bitcast.8, ...), custom_call_target="tpu_custom_call" | custom-call | tf_op jit(solution)/shard_map/pallas_call | solution.py:269
  39.0 0.7 %copy.11 = bf16[32,16,128]{2,1,0:T(8,128)(2,1)} copy(bf16[32,16,128]{2,1,0:T(8,128)(2,1)S(1)} %shard_map.91) | data formatting | bytes 262144

commit v6 on v5

--- a/solution.py
+++ b/solution.py
@@ -134,11 +134,16 @@
                 own[ch, wave, xx, top] = piece
                 xsend[ch, wave, xx, top] = piece.astype(BF16)
 
-    def send_along_x(ch, wave, d):
-        pltpu.make_async_remote_copy(
-            xsend.at[ch, wave, (x + d) % 4], xrecv.at[ch, wave, d - 1], sx.at[ch, wave, d - 1], rx.at[ch, wave, d - 1],
-            device_id=along_x(d), device_id_type=MESH,
-        ).start()
+    def send_along_x(ch, wave, top):
+        for d in (2, 1, 3):
+            pltpu.make_async_remote_copy(
+                xsend.at[ch, wave, (x + d) % 4, top], xrecv.at[ch, wave, d - 1, top], sx.at[ch, wave, top, d - 1],
+                rx.at[ch, wave, top, d - 1], device_id=along_x(d), device_id_type=MESH,
+            ).start()
+
+    def sent_along_x(ch, wave, top):
+        for d in range(3):
+            pltpu.make_async_copy(xsend.at[ch, wave, d, top], xsend.at[ch, wave, d, top], sx.at[ch, wave, top, d]).wait()
 
     for ch in range(2):
         pltpu.make_async_copy(recv1.at[ch, pl.ds(0, 63)], recv1.at[ch, pl.ds(0, 63)], r1.at[ch]).wait()
@@ -151,9 +156,9 @@
                 sides[0].append(jnp.where(low, one, pltpu.roll(two, 4, 0)))
                 sides[1].append(jnp.where(low, pltpu.roll(one, 4, 0), two))
             for group in range(4):
-                outs = exchange_blocks([sides[0][4 * group + a] for a in range(4)])
+                outs = exchange_blocks([sides[0][8 * (a // 2) + 2 * group + a % 2] for a in range(4)])
                 for h in range(2):
-                    left[ch, group % 2, at[h], pl.ds(group // 2 * 128, 128)] = jnp.concatenate(
+                    left[ch, group // 2, at[h], pl.ds(group % 2 * 128, 128)] = jnp.concatenate(
                         [outs[2 * h], outs[2 * h + 1]], axis=0
                     ).astype(BF16)
             for xpair in range(2):
@@ -186,22 +191,25 @@
                 at = ((xx // 2 * 4 + v) * 2 + xx % 2) * 16
                 rows[ch, xx * 64 + v * 16 : xx * 64 + v * 16 + 16, :] = turned[at : at + 16, :]
         partial_sums(ch, 0)
-        for d in (2, 1, 3):
-            send_along_x(ch, 0, d)
+        send_along_x(ch, 0, 0)
+        if ch == 0:
+            send_along_x(0, 0, 1)
     partial_sums(1, 1)
-    for ch in range(2):
-        for d in range(3):
-            pltpu.make_async_copy(xsend.at[ch, 0, d], xsend.at[ch, 0, d], sx.at[ch, 0, d]).wait()
-    for ch in range(2):
-        for d in (2, 1, 3):
-            send_along_x(ch, 1, d)
+    sent_along_x(0, 0, 0)
+    sent_along_x(0, 0, 1)
+    sent_along_x(1, 0, 0)
+    send_along_x(1, 0, 1)
+    sent_along_x(1, 0, 1)
+    for top in range(2):
+        for ch in range(2):
+            send_along_x(ch, 1, top)
 
     for wave in range(2):
-        for ch in range(2):
-            for d in range(3):
-                pltpu.make_async_copy(xrecv.at[ch, wave, d], xrecv.at[ch, wave, d], rx.at[ch, wave, d]).wait()
         for top in range(2):
-            q = top * 2 + wave
+            for ch in range(2):
+                for d in range(3):
+                    arrived = xrecv.at[ch, wave, d, top]
+                    pltpu.make_async_copy(arrived, arrived, rx.at[ch, wave, top, d]).wait()
             totals = []
             for ch in range(2):
                 total = own[ch, wave, x, top]
@@ -211,25 +219,25 @@
             for v in range(4):
                 tiles = [totals[ch][v * 16 + s * 8 : v * 16 + s * 8 + 8, :] for ch in range(2) for s in range(2)]
                 for g, out in enumerate(exchange_blocks(tiles)):
-                    send3[q, g * 4 + v] = out.astype(BF16)
-
-            for n in range(16):
-                p = q * 16 + n
-
-                @pl.when(p != me)
-                def _(n=n, p=p, q=q):
-                    pltpu.make_async_remote_copy(
-                        send3.at[q, n], tri.at[me], s3, r3, device_id=plane(p), device_id_type=MESH
-                    ).start()
-
-    tri[me] = send3[gx // 4, me % 16]
+                    p = (g // 2 * 8 + wave * 4 + top * 2 + g % 2) * 4 + v
+                    send3[p] = out.astype(BF16)
+                for g in range(4):
+                    p = (g // 2 * 8 + wave * 4 + top * 2 + g % 2) * 4 + v
+
+                    @pl.when(me != p)
+                    def _(p=p):
+                        pltpu.make_async_remote_copy(
+                            send3.at[p], tri.at[me], s3, r3, device_id=plane(p), device_id_type=MESH
+                        ).start()
+
+    tri[me] = send3[me]
 
     gain = jnp.transpose(jnp.broadcast_to(out_gain[...], (128, 128)))
     bias = jnp.transpose(jnp.broadcast_to(out_bias[...], (128, 128)))
     for ch in range(2):
         pltpu.make_async_copy(send1.at[ch, pl.ds(0, 63)], send1.at[ch, pl.ds(0, 63)], s1.at[ch]).wait()
-        for d in range(3):
-            pltpu.make_async_copy(xsend.at[ch, 1, d], xsend.at[ch, 1, d], sx.at[ch, 1, d]).wait()
+        for top in range(2):
+            sent_along_x(ch, 1, top)
     pltpu.make_async_copy(tri.at[pl.ds(0, 63)], tri.at[pl.ds(0, 63)], r3).wait()
 
     wide[...] = tri[...].astype(F32).reshape(512, 128)
@@ -285,13 +293,13 @@
             vmem((2, 2, 4, 2, 64, 128), BF16),
             vmem((2, 2, 3, 2, 64, 128), BF16),
             vmem((2, 2, 4, 2, 64, 128), F32),
-            vmem((4, 16, 8, 128), BF16),
+            vmem((64, 8, 128), BF16),
             vmem((64, 8, 128), BF16),
             vmem((512, 128), F32),
             vmem((512, 128), F32),
             vmem((512, 128), F32),
             dma((9,)), dma((2,)), dma((2,)), dma((2,)), dma((2,)), dma((2,)), dma((2,)),
-            dma((2, 2, 3)), dma((2, 2, 3)), dma, dma,
+            dma((2, 2, 2, 3)), dma((2, 2, 2, 3)), dma, dma,
         ],
         compiler_params=pltpu.CompilerParams(collective_id=1, has_side_effects=True),
     )(*args)

time: 39.8 us -> 39.4 us (0.990)
  Pallas kernels: 39 us -> 38.3 us
    pallas_call x1, Pallas kernels: 39 us -> 38.3 us  [on_device(): pl.pallas_call(kernel, out_shape=pltpu.VMEM((32, 16, 128), BF16), in_spec...]
where the time goes in v6:
time: 39.4 us; the launch traced here: 39 us
  Pallas kernels  38.3 us (97%)
  local copies, waits for them, and re-layouts  0.66 us (2%)
    pallas_call x1, Pallas kernels, on_device(): pl.pallas_call(kernel, out_shape=pltpu.VMEM((32, 16, 128), BF16), in_spec...  38.3 us

profile of v6, /device:TPU:1, one launch (start us, length us, event | category | flops | bytes accessed | tf_op | source)
XLA Modules:
  0.0 39.0 jit_solution(6620140394683568988)
XLA Ops:
  0.0 38.3 %shard_map.91 = bf16[32,16,128]{2,1,0:T(8,128)(2,1)S(1)} custom-call(bf16[32,16,128]{2,1,0:T(8,128)(2,1)} %pair_hbm.1, s32[16,32]{1,0:T(8,128)} %bitcast.5, f32[1,128]{1,0:T(1,128)} %bitcast.6, f32[1,128]{1,0:T(1,128)} %bitcast.7, bf16[128,512]{1,0:T(8,128)(2,1)} %proj_hbm.1, bf16[128,128]{1,0:T(8,128)(2,1)} %gatew_hbm.1, f32[1,128]{1,0:T(1,128)} %bitcast.8, ...), custom_call_target="tpu_custom_call" | custom-call | tf_op jit(solution)/shard_map/pallas_call | solution.py:277
  38.3 0.7 %copy.11 = bf16[32,16,128]{2,1,0:T(8,128)(2,1)} copy(bf16[32,16,128]{2,1,0:T(8,128)(2,1)S(1)} %shard_map.91) | data formatting | bytes 262144
